TPU v7x, 256 devices: a whole 4x4x8 slice. The times are simulated.
256 devices in a mesh: expert: 64 (over x, z, core), pair: 2 (over y_lo), dp: 2 (over y_hi).
Axes of the slice: x: 4, y: 4 (y_hi: 2, y_lo: 2; y = y_hi * 2 + y_lo), z: 8, core: 2. Of those that a mesh axis runs over, the one named last changes fastest.
Arguments:
- tokens: bfloat16 [1024, 196, 768], P(('expert', 'pair', 'dp')), may hold values from -96 to 96
- phi: bfloat16 [768, 128], replicated, may hold values from -0.25 to 0.25
- w_in: bfloat16 [64, 768, 3072], P('expert', None, 'pair'), may hold values from -0.21875 to 0.21875
- w_out: bfloat16 [64, 3072, 768], P('expert', 'pair'), may hold values from -0.109375 to 0.109375
- slot_out: bfloat16 [1024, 128, 768], P(('expert', 'pair', 'dp')), may hold values from -6 to 6
- grad_out: bfloat16 [1024, 196, 768], P(('expert', 'pair', 'dp')), may hold values from -6 to 6
Outputs:
- token_grad: bfloat16 [1024, 196, 768], P(('expert', 'pair', 'dp'))
- phi_grad: float32 [768, 128], replicated
- grad_w_in: bfloat16 [64, 768, 3072], P('expert', 'dp', 'pair')
- grad_w_out: bfloat16 [64, 3072, 768], P('expert', 'pair', 'dp')
All inputs are finite; a program needn't handle non-finite values.
Results may differ from a plain program's by a relative error of at most 0.0086.
Values may be sent and summed in bfloat16 or wider, within the bound.
No kernel may reach another device: no remote copies, remote signals or barrier semaphores. Data moves between devices by JAX's collectives and lax.ppermute only.
A program may use at most 128 MiB of HBM per device.

v0:
```python
import jax
import jax.numpy as jnp
from jax import lax
from jax.sharding import PartitionSpec as P


def in_blocks(array, dim, peers):
    dims = array.shape
    pieces = array.reshape(*dims[:dim], peers, dims[dim] // peers, *dims[dim + 1 :])
    return jnp.moveaxis(pieces, dim, 0)


def sum_at_owner(array, axis, dim):
    pieces = in_blocks(array, dim, lax.axis_size(axis))
    arrived = lax.all_to_all(pieces, axis, split_axis=0, concat_axis=0, tiled=True)
    return arrived.sum(axis=0)


def summed_on_arrival(array, axis, dim):
    peers = lax.axis_size(axis)
    pieces = lax.all_to_all(in_blocks(array, dim, peers), axis, 0, 0, tiled=True)
    return jnp.sum(pieces.astype(jnp.float32), axis=0)


def expert_rows(z_rows, g_rows, w_first, w_second):
    pre = jnp.dot(z_rows, w_first, preferred_element_type=jnp.float32)
    act_full, gelu_back = jax.vjp(jax.nn.gelu, pre)
    act = act_full.astype(jnp.bfloat16)
    dact = lax.dot_general(
        g_rows, w_second, (((1,), (1,)), ((), ())), preferred_element_type=jnp.float32
    )
    dpre = gelu_back(dact)[0].astype(jnp.bfloat16)
    grad_second = lax.dot_general(
        act, g_rows, (((0,), (0,)), ((), ())), preferred_element_type=jnp.float32
    )
    grad_first = lax.dot_general(
        z_rows, dpre, (((0,), (0,)), ((), ())), preferred_element_type=jnp.float32
    )
    back = lax.dot_general(
        dpre, w_first, (((1,), (1,)), ((), ())), preferred_element_type=jnp.float32
    )
    return (grad_first, grad_second, back)


def local(tokens, phi, w_in, w_out, slot_out, grad_out):
    f32 = jnp.float32
    images, _, width = tokens.shape
    groups = lax.axis_size("expert")
    per_group = phi.shape[1] // groups
    experts_here = w_in.shape[0]
    slots = per_group // experts_here
    logits = jnp.einsum("bmd,ds->bms", tokens, phi, preferred_element_type=f32)
    dispatch = jax.nn.softmax(logits, axis=1)
    combine = jax.nn.softmax(logits, axis=2)
    dispatch_low = dispatch.astype(jnp.bfloat16)
    combine_low = combine.astype(jnp.bfloat16)
    slot_in = jnp.einsum("bms,bmd->bsd", dispatch_low, tokens, preferred_element_type=f32).astype(
        jnp.bfloat16
    )
    slot_grad = jnp.einsum(
        "bms,bmd->bsd", combine_low, grad_out, preferred_element_type=f32
    ).astype(jnp.bfloat16)
    outgoing_in = slot_in.reshape(images, groups, per_group, width)
    outgoing_grad = slot_grad.reshape(images, groups, per_group, width)
    arrived_in, arrived_grad = (
        lax.all_to_all(outgoing_in, "expert", split_axis=1, concat_axis=0, tiled=True),
        lax.all_to_all(outgoing_grad, "expert", split_axis=1, concat_axis=0, tiled=True),
    )
    rows_in, rows_grad = (
        lax.all_gather(arrived_in, "pair", axis=0, tiled=True),
        lax.all_gather(arrived_grad, "pair", axis=0, tiled=True),
    )
    count = rows_in.shape[0]
    z_rows = rows_in[:, 0].reshape(count * slots, width)
    g_rows = rows_grad[:, 0].reshape(count * slots, width)
    grad_first, grad_second, back = expert_rows(z_rows, g_rows, w_in[0], w_out[0])
    firsts = [grad_first]
    seconds = [grad_second]
    backs = back.reshape(count, 1, slots, width)
    back_sum = sum_at_owner(backs, "pair", 0)
    grad_w_in = lax.psum_scatter(
        jnp.stack(firsts).astype(jnp.bfloat16), "dp", scatter_dimension=1, tiled=True
    )
    grad_w_out = summed_on_arrival(jnp.stack(seconds).astype(jnp.bfloat16), "dp", 2).astype(
        jnp.bfloat16
    )
    back_low = back_sum.astype(jnp.bfloat16)
    returned = lax.all_to_all(back_low, "expert", split_axis=0, concat_axis=1, tiled=True)
    slot_in_grad = returned.reshape(images, groups * per_group, width)
    dispatch_grad = jnp.einsum("bmd,bsd->bms", tokens, slot_in_grad, preferred_element_type=f32)
    combine_grad = jnp.einsum("bmd,bsd->bms", grad_out, slot_out, preferred_element_type=f32)
    logit_grad = dispatch * (
        dispatch_grad - jnp.sum(dispatch * dispatch_grad, axis=1, keepdims=True)
    )
    logit_grad = logit_grad + combine * (
        combine_grad - jnp.sum(combine * combine_grad, axis=2, keepdims=True)
    )
    logit_low = logit_grad.astype(jnp.bfloat16)
    token_part = jnp.einsum("bms,bsd->bmd", dispatch_low, slot_in_grad, preferred_element_type=f32)
    token_grad = (
        token_part + jnp.einsum("bms,ds->bmd", logit_low, phi, preferred_element_type=f32)
    ).astype(jnp.bfloat16)
    phi_part = jnp.einsum("bmd,bms->ds", tokens, logit_low, preferred_element_type=f32)
    phi_grad = lax.psum(phi_part, ("expert", "pair", "dp"))
    return (token_grad, phi_grad, grad_w_in, grad_w_out)


def solution(mesh):
    in_specs = (
        P(("expert", "pair", "dp"), None, None),
        P(),
        P("expert", None, "pair"),
        P("expert", "pair", None),
        P(("expert", "pair", "dp"), None, None),
        P(("expert", "pair", "dp"), None, None),
    )
    out_specs = (
        P(("expert", "pair", "dp"), None, None),
        P(),
        P("expert", "dp", "pair"),
        P("expert", "pair", "dp"),
    )
    return jax.shard_map(local, mesh=mesh, in_specs=in_specs, out_specs=out_specs, check_vma=False)
```

profile of v0, /device:TPU:1, one launch (start us, length us, event | category | flops | bytes accessed | tf_op | source)
XLA Modules:
  0.0 530.7 jit_solution(16438834560802032734)
XLA Ops:
  7.2 1.9 fusion.46
  9.1 0.9 fusion.64
  10.0 0.6 copy-done.7
  10.6 2.7 convolution_convert_fusion.2
  13.3 2.2 reshape.48
  15.4 1.4 copy.36
  16.8 13.0 %all-to-all-start.1 = ((bf16[4,64,2,768]{3,2,0,1:T(2,128)(2,1)}), bf16[4,64,2,768]{3,2,0,1:T(2,128)(2,1)S(1)}, u32[]{:S(2)}, u32[]{:S(2)}) async-start(bf16[4,64,2,768]{3,2,0,1:T(2,128)(2,1)} %copy.36), calls=%async_computation.1 | async-start | bytes 1572864 | tf_op jit(solution)/shard_map/all_to_all | solution.py:66
  29.8 0.0 all-gather.5.cloned.1.call-start
  29.9 1.6 fusion.65
  31.4 21.3 %all-to-all-done.1 = bf16[4,64,2,768]{3,2,0,1:T(2,128)(2,1)S(1)} async-done(((bf16[4,64,2,768]{3,2,0,1:T(2,128)(2,1)}), bf16[4,64,2,768]{3,2,0,1:T(2,128)(2,1)S(1)}, u32[]{:S(2)}, u32[]{:S(2)}) %all-to-all-start.1) | async-done | bytes 786464 | tf_op jit(solution)/shard_map/all_to_all | solution.py:66
  52.7 0.9 copy-done.1
  53.6 0.0 all-gather.3.cloned.1.call-start
  53.7 3.9 convolution_convert_fusion.3
  57.6 2.2 reshape.47
  59.8 0.5 copy.33
  60.3 29.1 %all_to_all.61 = bf16[4,64,2,768]{3,2,0,1:T(2,128)(2,1)} all-to-all(bf16[4,64,2,768]{3,2,0,1:T(2,128)(2,1)S(1)} %copy.33), channel_id=1, replica_groups=mesh['expert'=64,'pair'=2,'dp'=2] {'expert'}, dimensions={1} | all-to-all | bytes 1572864 | tf_op jit(solution)/shard_map/all_to_all | solution.py:67
  89.4 0.0 all-gather.5.cloned.1.call-done
  89.4 4.6 reshape_squeeze.7
  94.1 5.9 %fusion.18 = f32[1024,1536]{1,0:T(8,128)} fusion(bf16[1024,768]{1,0:T(8,128)(2,1)} %reshape_squeeze.7, bf16[1,768,1536]{2,1,0:T(8,128)(2,1)S(1)} %copy-done), kind=kOutput, calls=%fused_computation.26 | convolution fusion | flops 2415919104 | bytes 10223616 | tf_op jit(solution)/shard_map/dot_general | solution.py:26
  100.0 18.7 %all-gather.3.cloned.1.call-done = bf16[512,1,2,768]{3,2,1,0:T(2,128)(2,1)} async-done(((bf16[256,1,2,768]{3,2,1,0:T(2,128)(2,1)}), bf16[512,1,2,768]{3,2,1,0:T(2,128)(2,1)}) %all-gather.3.cloned.1.call-update) | async-done | bytes 1572880 | tf_op jit(solution)/shard_map/all_gather | solution.py:71
  118.7 4.7 reshape_squeeze.6
  123.4 9.6 %fusion.10 = bf16[1024,1536]{1,0:T(8,128)(2,1)} fusion(f32[1024,1536]{1,0:T(8,128)} %fusion.18, bf16[1024,768]{1,0:T(8,128)(2,1)} %reshape_squeeze.6, bf16[1,1536,768]{2,1,0:T(8,128)(2,1)} %param.9), kind=kOutput, calls=%fused_computation.12 | convolution fusion | flops 2447376384 | bytes 13369344 | tf_op jit(solution)/shard_map/dot_general | solution.py:29
  133.0 7.2 %reshape.49 = bf16[2,256,2,1536]{3,2,1,0:T(2,128)(2,1)} reshape(bf16[1024,1536]{1,0:T(8,128)(2,1)} %fusion.10) | data formatting | bytes 6291456 | tf_op jit(solution)/shard_map/reshape.20
  140.2 4.5 fusion.24
  144.7 38.0 %all_to_all.62 = f32[2,256,1,2,768]{4,1,3,2,0:T(8,128)S(1)} all-to-all(f32[2,256,1,2,768]{4,1,3,2,0:T(8,128)S(1)} %fusion.24), channel_id=1, replica_groups=mesh['expert'=64,'pair'=2,'dp'=2] {'pair'}, dimensions={0} | all-to-all | bytes 6291456 | tf_op jit(solution)/shard_map/all_to_all | solution.py:15
  182.7 0.2 bitcast_reduce_fusion
  182.9 1.7 copy.41
  184.6 11.7 %all-to-all-start.3 = ((bf16[256,1,2,768]{3,2,1,0:T(2,128)(2,1)}), bf16[256,1,2,768]{3,2,1,0:T(2,128)(2,1)S(1)}, u32[]{:S(2)}, u32[]{:S(2)}) async-start(bf16[256,1,2,768]{3,2,1,0:T(2,128)(2,1)} %copy.41), calls=%async_computation.3 | async-start | bytes 1572864 | tf_op jit(solution)/shard_map/all_to_all | solution.py:88
  196.3 0.0 all-reduce.2.cloned.1.call-start
  196.3 2.7 fusion.39
  199.1 20.1 %all-to-all-done.3 = bf16[256,1,2,768]{3,2,1,0:T(2,128)(2,1)S(1)} async-done(((bf16[256,1,2,768]{3,2,1,0:T(2,128)(2,1)}), bf16[256,1,2,768]{3,2,1,0:T(2,128)(2,1)S(1)}, u32[]{:S(2)}, u32[]{:S(2)}) %all-to-all-start.3) | async-done | bytes 786464 | tf_op jit(solution)/shard_map/all_to_all | solution.py:88
  219.2 1.4 copy.42
  220.6 2.3 reshape.50
  223.0 2.0 convolution_bitcast_fusion
  225.0 0.9 fusion.37
  225.9 6.8 %convolution_bitcast_fusion.1 = f32[768,128]{0,1:T(8,128)} fusion(f32[4,196,128]{2,1,0:T(8,128)} %fusion.37, f32[4,196,128]{2,1,0:T(8,128)} %fusion.39, bf16[4,196,768]{2,0,1:T(4,128)(2,1)} %param.6, f32[4,196,128]{2,1,0:T(8,128)} %get-tuple-element.19, f32[4,196]{1,0:T(4,128)} %get-tuple-element.18), kind=kOutput, calls=%fused_computation.43 | convolution fusion | flops 154844048 | bytes 2804800 | tf_op jit(solution)/shard_map/bmd,bms->ds/dot_general | solution.py:103
  232.8 0.0 reduce-scatter.2.cloned.1.call-start
  232.8 6.4 %fusion.16 = bf16[1,768,1536]{2,1,0:T(8,128)(2,1)} fusion(bf16[1024,768]{1,0:T(8,128)(2,1)} %reshape_squeeze.7, bf16[1024,1536]{1,0:T(8,128)(2,1)} %fusion.10), kind=kOutput, calls=%fused_computation.22 | convolution fusion | flops 2417098752 | bytes 7077888 | tf_op jit(solution)/shard_map/dot_general | solution.py:36
  239.2 6.2 %convolution_convert_fusion = bf16[1536,768]{0,1:T(8,128)(2,1)S(1)} fusion(bf16[1024,768]{1,0:T(8,128)(2,1)} %reshape_squeeze.6, f32[1024,1536]{1,0:T(8,128)} %fusion.18), kind=kOutput, calls=%fused_computation.14 | convolution fusion | flops 2431254528 | bytes 10223616 | tf_op jit(solution)/shard_map/dot_general | solution.py:33
  245.4 32.5 %all_to_all.63 = bf16[2,1,1536,384]{2,3,1,0:T(8,128)(2,1)S(1)} all-to-all(bf16[2,1,1536,384]{2,3,1,0:T(8,128)(2,1)S(1)} %bitcast.83), channel_id=1, replica_groups=mesh['expert'=64,'pair'=2,'dp'=2] {'dp'}, dimensions={0} | all-to-all | bytes 4718592 | tf_op jit(solution)/shard_map/all_to_all | solution.py:21
  277.9 0.4 bitcast_reduce_fusion.1
  278.3 1.4 copy.50
  279.7 6.9 %fusion.42 = f32[4,196,768]{2,1,0:T(8,128)} fusion(f32[4,196,128]{2,1,0:T(8,128)} %fusion.37, f32[4,196,128]{2,1,0:T(8,128)} %fusion.39, bf16[768,128]{1,0:T(8,128)(2,1)} %param.7, f32[4,196,128]{2,1,0:T(8,128)} %get-tuple-element.19, f32[4,196]{1,0:T(4,128)S(1)} %copy-done.6), kind=kOutput, calls=%fused_computation.48 | convolution fusion | flops 154844048 | bytes 3812416 | tf_op jit(solution)/shard_map/bms,ds->bmd/dot_general | solution.py:101
  286.6 3.5 add_convert_fusion
  290.2 2.8 copy.48
  292.9 188.6 %all-reduce.2.cloned.1.call-done = f32[768,128]{0,1:T(8,128)} async-done(((f32[768,128]{0,1:T(8,128)}), f32[768,128]{0,1:T(8,128)}) %all-reduce.2.cloned.1.call-update) | async-done | bytes 393232 | tf_op jit(solution)/shard_map/psum | solution.py:104
  481.6 1.9 copy.49
  483.5 40.7 %reduce-scatter.2.cloned.1.call-done = bf16[1,384,1536]{2,1,0:T(8,128)(2,1)} async-done(((bf16[1,768,1536]{2,1,0:T(8,128)(2,1)}), bf16[1,384,1536]{2,1,0:T(8,128)(2,1)}) %reduce-scatter.2.cloned.1.call-update) | async-done | bytes 1179664 | tf_op jit(solution)/shard_map/reduce_scatter | solution.py:81
  (22 shorter events, 0.1 us)
Async XLA Ops:
  7.2 86.9 %copy-start = (bf16[1,768,1536]{2,1,0:T(8,128)(2,1)S(1)}, bf16[1,768,1536]{2,1,0:T(8,128)(2,1)}, u32[]{:S(2)}) copy-start(bf16[1,768,1536]{2,1,0:T(8,128)(2,1)} %param.8) | copy-start | bytes 7077892
  9.1 44.6 %copy-start.4 = (f32[4,196,128]{2,1,0:T(8,128)}, f32[4,196,128]{2,1,0:T(8,128)S(1)}, u32[]{:S(2)}) copy-start(f32[4,196,128]{2,1,0:T(8,128)S(1)} %fusion.46) | copy-start | bytes 1204228
  10.0 0.6 copy-start.7
  16.8 35.9 %all-to-all-start.1 = ((bf16[4,64,2,768]{3,2,0,1:T(2,128)(2,1)}), bf16[4,64,2,768]{3,2,0,1:T(2,128)(2,1)S(1)}, u32[]{:S(2)}, u32[]{:S(2)}) async-start(bf16[4,64,2,768]{3,2,0,1:T(2,128)(2,1)} %copy.36), calls=%async_computation.1 | async-start | bytes 1572864 | tf_op jit(solution)/shard_map/all_to_all | solution.py:66
  29.8 59.6 %all-gather.5.cloned.1.call-start = ((), (), s32[]{:S(2)}) async-start(), calls=%async_computation.7 | async-start | bytes 2359296 | tf_op jit(solution)/shard_map/all_gather | solution.py:70
  52.7 0.9 copy-start.1
  53.6 65.0 %all-gather.3.cloned.1.call-start = ((), (), s32[]{:S(2)}) async-start(), calls=%async_computation.6 | async-start | bytes 2359296 | tf_op jit(solution)/shard_map/all_gather | solution.py:71
  184.6 34.6 %all-to-all-start.3 = ((bf16[256,1,2,768]{3,2,1,0:T(2,128)(2,1)}), bf16[256,1,2,768]{3,2,1,0:T(2,128)(2,1)S(1)}, u32[]{:S(2)}, u32[]{:S(2)}) async-start(bf16[256,1,2,768]{3,2,1,0:T(2,128)(2,1)} %copy.41), calls=%async_computation.3 | async-start | bytes 1572864 | tf_op jit(solution)/shard_map/all_to_all | solution.py:88
  196.3 285.3 %all-reduce.2.cloned.1.call-start = ((), (), s32[]{:S(2)}) async-start(), calls=%async_computation.8 | async-start | bytes 786432 | tf_op jit(solution)/shard_map/psum | solution.py:104
  220.6 4.4 copy-start.5
  222.9 3.0 copy-start.2
  222.9 2.1 copy-start.8
  232.8 291.4 %reduce-scatter.2.cloned.1.call-start = ((), (), s32[]{:S(2)}) async-start(), calls=%async_computation.9 | async-start | bytes 3538944 | tf_op jit(solution)/shard_map/reduce_scatter | solution.py:81
  277.9 1.8 copy-start.6
  278.3 8.4 %copy-start.9 = (f32[4,128]{1,0:T(4,128)S(1)}, f32[4,128]{1,0:T(4,128)}, u32[]{:S(2)}) copy-start(f32[4,128]{1,0:T(4,128)} %copy-done.7) | copy-start | bytes 6148
  279.7 6.9 %copy-start.3 = (bf16[4,128,768]{2,1,0:T(8,128)(2,1)S(1)}, bf16[4,128,768]{2,1,0:T(8,128)(2,1)}, u32[]{:S(2)}) copy-start(bf16[4,128,768]{2,1,0:T(8,128)(2,1)} %copy-done.2) | copy-start | bytes 2359300
Sparse Core Ops, SparseCore 0:
  53.8 29.1 all-gather.4
  89.5 29.1 all-gather.2
  232.9 248.6 all-reduce.1
  484.5 39.6 reduce-scatter.1
where the time goes:
time: 532 us; the launch traced here: 531 us
  waiting for transfers between devices  290 us (55%)
  blocking collectives  99.5 us (19%)
  matrix products  63.2 us (12%)
  local copies, waits for them, and re-layouts  35.8 us (7%)
  starting transfers between devices  24.8 us (5%)
  between operations  13.9 us (3%)
    psum x1, waiting for transfers between devices, local(): phi_grad = lax.psum(phi_part, ('expert', 'pair', 'dp'))  189 us
    reduce_scatter x1, waiting for transfers between devices, local(): lax.psum_scatter(jnp.stack(firsts).astype(jnp.bfloat16), 'dp', scatter_di...  40.7 us
    all_to_all x1, blocking collectives, sum_at_owner(): lax.all_to_all(pieces, axis, split_axis=0, concat_axis=0, tiled=True)  38 us
    all_to_all x1, blocking collectives, summed_on_arrival(): lax.all_to_all(in_blocks(array, dim, peers), axis, 0, 0, tiled=True)  32.5 us
    all_to_all x1, blocking collectives, local(): lax.all_to_all(outgoing_grad, 'expert', split_axis=1, concat_axis=0, tile...  29.1 us
    all_to_all x1, waiting for transfers between devices, local(): lax.all_to_all(outgoing_in, 'expert', split_axis=1, concat_axis=0, tiled=...  21.3 us
    all_to_all x1, waiting for transfers between devices, local(): lax.all_to_all(back_low, 'expert', split_axis=0, concat_axis=1, tiled=True)  20.1 us
    all_gather x1, waiting for transfers between devices, local(): lax.all_gather(arrived_grad, 'pair', axis=0, tiled=True)  18.7 us
  transfers between devices with their start and end apart: 6, of which 5 were waited for; matrix products, arithmetic and copies ran while one was open for 10% of the time, Pallas kernels for 0%

commit v1 on v0

--- a/solution.py
+++ b/solution.py
@@ -101,7 +101,8 @@
         token_part + jnp.einsum("bms,ds->bmd", logit_low, phi, preferred_element_type=f32)
     ).astype(jnp.bfloat16)
     phi_part = jnp.einsum("bmd,bms->ds", tokens, logit_low, preferred_element_type=f32)
-    phi_grad = lax.psum(phi_part, ("expert", "pair", "dp"))
+    inner = lax.psum(phi_part, ("pair", "dp"))
+    phi_grad = lax.psum(inner, "expert")
     return (token_grad, phi_grad, grad_w_in, grad_w_out)
 
 

time: 532 us -> 514 us (0.966)
  waiting for transfers between devices: 290 us -> 275 us
    psum x1 -> x2, waiting for transfers between devices: 189 us -> 172 us  [the longest x1 130 us: local(): phi_grad = lax.psum(inner, 'expert')]
  transfers between devices with their start and end apart: 6 -> 7, of which waited for: 5 -> 6; matrix products, arithmetic and copies ran while one was open for 10% -> 10% of each run, Pallas kernels for 0% -> 0%
where the time goes in v1:
time: 514 us; the launch traced here: 513 us
  waiting for transfers between devices  275 us (54%)
  blocking collectives  96.6 us (19%)
  matrix products  63.1 us (12%)
  local copies, waits for them, and re-layouts  35.8 us (7%)
  starting transfers between devices  24.9 us (5%)
  between operations  13.9 us (3%)
    psum x1, waiting for transfers between devices, local(): phi_grad = lax.psum(inner, 'expert')  130 us
    reduce_scatter x1, waiting for transfers between devices, local(): lax.psum_scatter(jnp.stack(firsts).astype(jnp.bfloat16), 'dp', scatter_di...  42.7 us
    psum x1, waiting for transfers between devices, local(): inner = lax.psum(phi_part, ('pair', 'dp'))  41.9 us
    all_to_all x1, blocking collectives, sum_at_owner(): lax.all_to_all(pieces, axis, split_axis=0, concat_axis=0, tiled=True)  38 us
    all_to_all x1, blocking collectives, summed_on_arrival(): lax.all_to_all(in_blocks(array, dim, peers), axis, 0, 0, tiled=True)  29.6 us
    all_to_all x1, blocking collectives, local(): lax.all_to_all(outgoing_grad, 'expert', split_axis=1, concat_axis=0, tile...  29.1 us
    all_to_all x1, waiting for transfers between devices, local(): lax.all_to_all(outgoing_in, 'expert', split_axis=1, concat_axis=0, tiled=...  21.3 us
    all_to_all x1, waiting for transfers between devices, local(): lax.all_to_all(back_low, 'expert', split_axis=0, concat_axis=1, tiled=True)  20.1 us
  transfers between devices with their start and end apart: 7, of which 6 were waited for; matrix products, arithmetic and copies ran while one was open for 10% of the time, Pallas kernels for 0%

profile of v1, /device:TPU:1, one launch (start us, length us, event | category | flops | bytes accessed | tf_op | source)
XLA Modules:
  0.0 513.4 jit_solution(12493824045756796472)
XLA Ops:
  7.2 1.9 fusion.46
  9.1 0.9 fusion.64
  10.0 0.6 copy-done.7
  10.6 2.7 convolution_convert_fusion.2
  13.3 2.2 reshape.48
  15.4 1.4 copy.36
  16.8 13.0 %all-to-all-start.1 = ((bf16[4,64,2,768]{3,2,0,1:T(2,128)(2,1)}), bf16[4,64,2,768]{3,2,0,1:T(2,128)(2,1)S(1)}, u32[]{:S(2)}, u32[]{:S(2)}) async-start(bf16[4,64,2,768]{3,2,0,1:T(2,128)(2,1)} %copy.36), calls=%async_computation.1 | async-start | bytes 1572864 | tf_op jit(solution)/shard_map/all_to_all | solution.py:66
  29.8 0.0 all-gather.5.cloned.1.call-start
  29.9 1.6 fusion.65
  31.4 21.3 %all-to-all-done.1 = bf16[4,64,2,768]{3,2,0,1:T(2,128)(2,1)S(1)} async-done(((bf16[4,64,2,768]{3,2,0,1:T(2,128)(2,1)}), bf16[4,64,2,768]{3,2,0,1:T(2,128)(2,1)S(1)}, u32[]{:S(2)}, u32[]{:S(2)}) %all-to-all-start.1) | async-done | bytes 786464 | tf_op jit(solution)/shard_map/all_to_all | solution.py:66
  52.8 0.9 copy-done.1
  53.7 0.0 all-gather.3.cloned.1.call-start
  53.7 3.9 convolution_convert_fusion.3
  57.6 2.2 reshape.47
  59.8 0.5 copy.33
  60.3 29.1 %all_to_all.61 = bf16[4,64,2,768]{3,2,0,1:T(2,128)(2,1)} all-to-all(bf16[4,64,2,768]{3,2,0,1:T(2,128)(2,1)S(1)} %copy.33), channel_id=1, replica_groups=mesh['expert'=64,'pair'=2,'dp'=2] {'expert'}, dimensions={1} | all-to-all | bytes 1572864 | tf_op jit(solution)/shard_map/all_to_all | solution.py:67
  89.4 4.6 reshape_squeeze.7
  94.1 5.9 %fusion.18 = f32[1024,1536]{1,0:T(8,128)} fusion(bf16[1024,768]{1,0:T(8,128)(2,1)} %reshape_squeeze.7, bf16[1,768,1536]{2,1,0:T(8,128)(2,1)S(1)} %copy-done), kind=kOutput, calls=%fused_computation.26 | convolution fusion | flops 2415919104 | bytes 10223616 | tf_op jit(solution)/shard_map/dot_general | solution.py:26
  100.0 18.7 %all-gather.3.cloned.1.call-done = bf16[512,1,2,768]{3,2,1,0:T(2,128)(2,1)} async-done(((bf16[256,1,2,768]{3,2,1,0:T(2,128)(2,1)}), bf16[512,1,2,768]{3,2,1,0:T(2,128)(2,1)}) %all-gather.3.cloned.1.call-update) | async-done | bytes 1572880 | tf_op jit(solution)/shard_map/all_gather | solution.py:71
  118.7 4.7 reshape_squeeze.6
  123.4 9.6 %fusion.10 = bf16[1024,1536]{1,0:T(8,128)(2,1)} fusion(f32[1024,1536]{1,0:T(8,128)} %fusion.18, bf16[1024,768]{1,0:T(8,128)(2,1)} %reshape_squeeze.6, bf16[1,1536,768]{2,1,0:T(8,128)(2,1)} %param.9), kind=kOutput, calls=%fused_computation.12 | convolution fusion | flops 2447376384 | bytes 13369344 | tf_op jit(solution)/shard_map/dot_general | solution.py:29
  133.0 7.2 %reshape.49 = bf16[2,256,2,1536]{3,2,1,0:T(2,128)(2,1)} reshape(bf16[1024,1536]{1,0:T(8,128)(2,1)} %fusion.10) | data formatting | bytes 6291456 | tf_op jit(solution)/shard_map/reshape.20
  140.2 4.5 fusion.24
  144.7 38.0 %all_to_all.62 = f32[2,256,1,2,768]{4,1,3,2,0:T(8,128)S(1)} all-to-all(f32[2,256,1,2,768]{4,1,3,2,0:T(8,128)S(1)} %fusion.24), channel_id=1, replica_groups=mesh['expert'=64,'pair'=2,'dp'=2] {'pair'}, dimensions={0} | all-to-all | bytes 6291456 | tf_op jit(solution)/shard_map/all_to_all | solution.py:15
  182.7 0.2 bitcast_reduce_fusion
  182.9 1.7 copy.41
  184.6 11.7 %all-to-all-start.3 = ((bf16[256,1,2,768]{3,2,1,0:T(2,128)(2,1)}), bf16[256,1,2,768]{3,2,1,0:T(2,128)(2,1)S(1)}, u32[]{:S(2)}, u32[]{:S(2)}) async-start(bf16[256,1,2,768]{3,2,1,0:T(2,128)(2,1)} %copy.41), calls=%async_computation.3 | async-start | bytes 1572864 | tf_op jit(solution)/shard_map/all_to_all | solution.py:88
  196.3 0.0 all-reduce.3.cloned.1.call-start
  196.3 2.7 fusion.39
  199.1 20.1 %all-to-all-done.3 = bf16[256,1,2,768]{3,2,1,0:T(2,128)(2,1)S(1)} async-done(((bf16[256,1,2,768]{3,2,1,0:T(2,128)(2,1)}), bf16[256,1,2,768]{3,2,1,0:T(2,128)(2,1)S(1)}, u32[]{:S(2)}, u32[]{:S(2)}) %all-to-all-start.3) | async-done | bytes 786464 | tf_op jit(solution)/shard_map/all_to_all | solution.py:88
  219.2 1.4 copy.42
  220.6 2.3 reshape.50
  223.0 2.0 convolution_bitcast_fusion
  225.0 0.9 fusion.37
  225.9 6.8 %convolution_bitcast_fusion.1 = f32[768,128]{0,1:T(8,128)} fusion(f32[4,196,128]{2,1,0:T(8,128)} %fusion.37, f32[4,196,128]{2,1,0:T(8,128)} %fusion.39, bf16[4,196,768]{2,0,1:T(4,128)(2,1)} %param.6, f32[4,196,128]{2,1,0:T(8,128)} %get-tuple-element.19, f32[4,196]{1,0:T(4,128)} %get-tuple-element.18), kind=kOutput, calls=%fused_computation.43 | convolution fusion | flops 154844048 | bytes 2804800 | tf_op jit(solution)/shard_map/bmd,bms->ds/dot_general | solution.py:103
  232.8 0.0 all-reduce.5.cloned.1.call-start
  232.8 41.9 %all-reduce.3.cloned.1.call-done = f32[768,128]{0,1:T(8,128)} async-done(((f32[768,128]{0,1:T(8,128)}), f32[768,128]{0,1:T(8,128)}) %all-reduce.3.cloned.1.call-update) | async-done | bytes 393232 | tf_op jit(solution)/shard_map/psum | solution.py:104
  274.8 6.4 %fusion.16 = bf16[1,768,1536]{2,1,0:T(8,128)(2,1)} fusion(bf16[1024,768]{1,0:T(8,128)(2,1)} %reshape_squeeze.7, bf16[1024,1536]{1,0:T(8,128)(2,1)} %fusion.10), kind=kOutput, calls=%fused_computation.22 | convolution fusion | flops 2417098752 | bytes 7077888 | tf_op jit(solution)/shard_map/dot_general | solution.py:36
  281.3 6.1 %convolution_convert_fusion = bf16[1536,768]{0,1:T(8,128)(2,1)S(1)} fusion(bf16[1024,768]{1,0:T(8,128)(2,1)} %reshape_squeeze.6, f32[1024,1536]{1,0:T(8,128)} %fusion.18), kind=kOutput, calls=%fused_computation.14 | convolution fusion | flops 2431254528 | bytes 10223616 | tf_op jit(solution)/shard_map/dot_general | solution.py:33
  287.4 29.6 %all_to_all.63 = bf16[2,1,1536,384]{2,3,1,0:T(8,128)(2,1)S(1)} all-to-all(bf16[2,1,1536,384]{2,3,1,0:T(8,128)(2,1)S(1)} %bitcast.83), channel_id=1, replica_groups=mesh['expert'=64,'pair'=2,'dp'=2] {'dp'}, dimensions={0} | all-to-all | bytes 4718592 | tf_op jit(solution)/shard_map/all_to_all | solution.py:21
  317.0 0.4 bitcast_reduce_fusion.1
  317.4 1.4 copy.50
  318.8 6.9 %fusion.42 = f32[4,196,768]{2,1,0:T(8,128)} fusion(f32[4,196,128]{2,1,0:T(8,128)} %fusion.37, f32[4,196,128]{2,1,0:T(8,128)} %fusion.39, bf16[768,128]{1,0:T(8,128)(2,1)} %param.7, f32[4,196,128]{2,1,0:T(8,128)} %get-tuple-element.19, f32[4,196]{1,0:T(4,128)S(1)} %copy-done.6), kind=kOutput, calls=%fused_computation.48 | convolution fusion | flops 154844048 | bytes 3812416 | tf_op jit(solution)/shard_map/bms,ds->bmd/dot_general | solution.py:101
  325.8 3.5 add_convert_fusion
  329.3 2.8 copy.48
  332.1 130.2 %all-reduce.5.cloned.1.call-done = f32[768,128]{0,1:T(8,128)} async-done(((f32[768,128]{0,1:T(8,128)}), f32[768,128]{0,1:T(8,128)}) %all-reduce.5.cloned.1.call-update) | async-done | bytes 393232 | tf_op jit(solution)/shard_map/psum | solution.py:105
  462.3 1.9 copy.49
  464.2 42.7 %reduce-scatter.2.cloned.1.call-done = bf16[1,384,1536]{2,1,0:T(8,128)(2,1)} async-done(((bf16[1,768,1536]{2,1,0:T(8,128)(2,1)}), bf16[1,384,1536]{2,1,0:T(8,128)(2,1)}) %reduce-scatter.2.cloned.1.call-update) | async-done | bytes 1179664 | tf_op jit(solution)/shard_map/reduce_scatter | solution.py:81
  (25 shorter events, 0.2 us)
Async XLA Ops:
  7.2 86.9 %copy-start = (bf16[1,768,1536]{2,1,0:T(8,128)(2,1)S(1)}, bf16[1,768,1536]{2,1,0:T(8,128)(2,1)}, u32[]{:S(2)}) copy-start(bf16[1,768,1536]{2,1,0:T(8,128)(2,1)} %param.8) | copy-start | bytes 7077892
  9.1 44.6 %copy-start.4 = (f32[4,196,128]{2,1,0:T(8,128)}, f32[4,196,128]{2,1,0:T(8,128)S(1)}, u32[]{:S(2)}) copy-start(f32[4,196,128]{2,1,0:T(8,128)S(1)} %fusion.46) | copy-start | bytes 1204228
  10.0 0.6 copy-start.7
  16.8 35.9 %all-to-all-start.1 = ((bf16[4,64,2,768]{3,2,0,1:T(2,128)(2,1)}), bf16[4,64,2,768]{3,2,0,1:T(2,128)(2,1)S(1)}, u32[]{:S(2)}, u32[]{:S(2)}) async-start(bf16[4,64,2,768]{3,2,0,1:T(2,128)(2,1)} %copy.36), calls=%async_computation.1 | async-start | bytes 1572864 | tf_op jit(solution)/shard_map/all_to_all | solution.py:66
  29.8 59.6 %all-gather.5.cloned.1.call-start = ((), (), s32[]{:S(2)}) async-start(), calls=%async_computation.7 | async-start | bytes 2359296 | tf_op jit(solution)/shard_map/all_gather | solution.py:70
  52.7 0.9 copy-start.1
  53.7 65.0 %all-gather.3.cloned.1.call-start = ((), (), s32[]{:S(2)}) async-start(), calls=%async_computation.6 | async-start | bytes 2359296 | tf_op jit(solution)/shard_map/all_gather | solution.py:71
  184.6 34.6 %all-to-all-start.3 = ((bf16[256,1,2,768]{3,2,1,0:T(2,128)(2,1)}), bf16[256,1,2,768]{3,2,1,0:T(2,128)(2,1)S(1)}, u32[]{:S(2)}, u32[]{:S(2)}) async-start(bf16[256,1,2,768]{3,2,1,0:T(2,128)(2,1)} %copy.41), calls=%async_computation.3 | async-start | bytes 1572864 | tf_op jit(solution)/shard_map/all_to_all | solution.py:88
  196.3 78.5 %all-reduce.3.cloned.1.call-start = ((), (), s32[]{:S(2)}) async-start(), calls=%async_computation.8 | async-start | bytes 786432 | tf_op jit(solution)/shard_map/psum | solution.py:104
  220.6 4.4 copy-start.5
  222.9 3.0 copy-start.2
  223.0 2.1 copy-start.8
  232.8 229.5 %all-reduce.5.cloned.1.call-start = ((), (), s32[]{:S(2)}) async-start(), calls=%async_computation.9 | async-start | bytes 786432 | tf_op jit(solution)/shard_map/psum | solution.py:105
  274.8 232.1 %reduce-scatter.2.cloned.1.call-start = ((), (), s32[]{:S(2)}) async-start(), calls=%async_computation.10 | async-start | bytes 3538944 | tf_op jit(solution)/shard_map/reduce_scatter | solution.py:81
  317.0 1.8 copy-start.6
  317.4 8.4 %copy-start.9 = (f32[4,128]{1,0:T(4,128)S(1)}, f32[4,128]{1,0:T(4,128)}, u32[]{:S(2)}) copy-start(f32[4,128]{1,0:T(4,128)} %copy-done.7) | copy-start | bytes 6148
  318.8 6.9 %copy-start.3 = (bf16[4,128,768]{2,1,0:T(8,128)(2,1)S(1)}, bf16[4,128,768]{2,1,0:T(8,128)(2,1)}, u32[]{:S(2)}) copy-start(bf16[4,128,768]{2,1,0:T(8,128)(2,1)} %copy-done.2) | copy-start | bytes 2359300
Sparse Core Ops, SparseCore 0:
  53.8 29.1 all-gather.4
  89.5 29.1 all-gather.2
  232.9 41.8 all-reduce.2
  278.1 184.1 all-reduce.4
  465.2 41.6 reduce-scatter.1
